TPU v7x, 32 devices: a whole 2x2x4 slice. The times are simulated.
32 devices in a mesh: groups: 2 (over x), rows: 8 (over z, y), cols: 2 (over core).
Axes of the slice: x: 2, y: 2, z: 4, core: 2. Of those that a mesh axis runs over, the one named last changes fastest.
Arguments:
- feature_table: float32 [32768, 1024], P(('groups', 'rows'), 'cols'), parts along dimension 0, may hold values from -6 to 6
- own_features: float32 [512, 1024], P(('groups', 'rows'), 'cols'), parts along dimension 0, may hold values from -6 to 6
- neighbor_ids: int32 [512, 50], P(('groups', 'rows')), parts along dimension 0, may hold values from 0 to 16383, as said below
- importance: float32 [512, 50], P(('groups', 'rows')), parts along dimension 0, may hold values from 0.5 to 5
- w_self: bfloat16 [1024, 1024], P('cols'), may hold values from -0.1875 to 0.1875
- w_pool: bfloat16 [1024, 1024], P('cols'), may hold values from -0.1875 to 0.1875
- bias: float32 [1024], replicated, may hold values from -6 to 6
Outputs:
- embeddings: float32 [512, 1024], P(('groups', 'rows'), 'cols'), parts along dimension 0
There are 2 independent parts, one for each index of `groups`. A program takes and returns all parts, laid end to end along the dimension named above; an argument that names none is the same for every part. Nothing has to cross between parts.
Inputs may be any that keep to these rules, and one draw needn't show every extreme that they name: `neighbor_ids`: ids of sampled neighbors in the group's table, repeats allowed. In each aligned block of 16 targets, at most 160 ids fall in any one range [k * 2048, (k + 1) * 2048), and one such range holds exactly 160.
All inputs are finite; a program needn't handle non-finite values.
Results may differ from a plain program's by a relative error of at most 0.0017.
Values may be sent and summed in bfloat16 or wider, within the bound.
A program may use at most 64 MiB of HBM per device.

v0:
```python
from functools import partial
import jax
import jax.numpy as jnp
from jax import lax
from jax.sharding import PartitionSpec as P

NEIGH = 50
TGT_DEV = 16


def request_slots(id_block, share_block, owners, capacity, rows_dev):
    targets = id_block.shape[0]
    neighbors = id_block.shape[1]
    flat_ids = id_block.reshape(-1)
    owner_of = flat_ids // rows_dev
    local_row = flat_ids - owner_of * rows_dev
    target_of = jnp.arange(targets * neighbors, dtype=jnp.int32) // neighbors
    onehot = (owner_of[:, None] == jnp.arange(owners, dtype=jnp.int32)[None, :]).astype(jnp.int32)
    slot_rank = jnp.sum((jnp.cumsum(onehot, axis=0) - onehot) * onehot, axis=1)
    sending = jnp.zeros((owners, capacity), jnp.int32).at[owner_of, slot_rank].set(local_row)
    packed = (
        jnp.zeros((owners, capacity), jnp.int32)
        .at[owner_of, slot_rank]
        .set(local_row * targets + target_of)
    )
    slot_weight = (
        jnp.zeros((owners, capacity), jnp.float32)
        .at[owner_of, slot_rank]
        .set(share_block.reshape(-1))
    )
    return (owner_of, slot_rank, sending, packed, slot_weight)


def plan_requests(id_rows, shares, blocks, owners, capacity, rows_dev):
    targets = id_rows.shape[0] // blocks
    neighbors = id_rows.shape[1]
    per_block = targets * neighbors
    owner_of, slot_rank, sending, packed, slot_weight = jax.vmap(
        partial(request_slots, owners=owners, capacity=capacity, rows_dev=rows_dev)
    )(id_rows.reshape(blocks, targets, neighbors), shares.reshape(blocks, targets, neighbors))
    block_of = jnp.arange(blocks, dtype=jnp.int32)[:, None]
    column = owner_of * (blocks * capacity) + block_of * capacity + slot_rank
    row_index = block_of * targets + jnp.arange(per_block, dtype=jnp.int32)[None, :] // neighbors
    pool_matrix = (
        jnp.zeros((blocks * targets, owners * blocks * capacity), jnp.float32)
        .at[row_index.reshape(-1), column.reshape(-1)]
        .add(shares.reshape(-1))
    )
    outgoing = jnp.transpose(sending, (1, 0, 2)).reshape(owners, blocks * capacity)
    packed_out = jnp.transpose(packed, (1, 0, 2)).reshape(owners, blocks * capacity)
    weight_out = jnp.transpose(slot_weight, (1, 0, 2)).reshape(owners, blocks * capacity)
    return (pool_matrix, outgoing, packed_out, weight_out)


def finish_rows(preact):
    hidden = jnp.maximum(preact, 0.0)
    return hidden * lax.rsqrt(jnp.mean(hidden * hidden, axis=1, keepdims=True) + 1e-06)


def body(feature_table, own_features, neighbor_ids, importance, w_self, w_pool, bias):
    rows_dev, width_half = feature_table.shape
    owners = lax.axis_size("rows")
    col_count = lax.axis_size("cols")
    capacity = TGT_DEV * NEIGH * 8 // (5 * owners)
    shares = importance / jnp.sum(importance, axis=1, keepdims=True)
    own_round = own_features.astype(jnp.bfloat16)
    pool_matrix, outgoing, packed_out, weight_out = plan_requests(
        neighbor_ids, shares, col_count, owners, capacity, rows_dev
    )
    found = jnp.take(
        feature_table,
        lax.all_to_all(outgoing, "rows", split_axis=0, concat_axis=0, tiled=True),
        axis=0,
    )
    arrived = lax.all_to_all(
        found.astype(jnp.bfloat16), "rows", split_axis=0, concat_axis=0, tiled=True
    ).astype(found.dtype)
    pooled = jnp.dot(
        pool_matrix,
        arrived.reshape(-1, width_half),
        precision=lax.Precision.HIGHEST,
        preferred_element_type=jnp.float32,
    )
    partial_sums = jnp.dot(own_round, w_self, preferred_element_type=jnp.float32) + jnp.dot(
        pooled.astype(jnp.bfloat16), w_pool, preferred_element_type=jnp.float32
    )
    column_start = lax.axis_index("cols") * width_half
    preact = lax.psum(partial_sums, "cols") + bias
    embedded = finish_rows(preact)
    return lax.dynamic_slice_in_dim(embedded, column_start, width_half, 1)


def solution(mesh):
    placed = (
        P(("groups", "rows"), "cols"),
        P(("groups", "rows"), "cols"),
        P(("groups", "rows"), None),
        P(("groups", "rows"), None),
        P("cols", None),
        P("cols", None),
        P(),
    )
    return jax.shard_map(
        body, mesh=mesh, in_specs=placed, out_specs=P(("groups", "rows"), "cols"), check_vma=False
    )
```

profile of v0, /device:TPU:0, one launch (start us, length us, event | category | flops | bytes accessed | tf_op | source)
XLA Modules:
  0.0 143.6 jit_solution(3626495202267903380)
XLA Ops:
  6.5 0.9 reshape_reshape.8
  7.4 0.8 reshape_reshape.9
  8.3 4.0 %reduce-window.6 = s32[2,8,7,128]{3,1,2,0:T(8,128)S(1)} reduce-window(s32[2,8,7,128]{3,1,2,0:T(8,128)S(1)} %convert_bitcast_fusion, s32[]{:T(128)} %constant.33.clone.1), window={size=1x1x1x128 pad=0_0x0_0x0_0x127_0}, to_apply=%region_0.0 | reduce-window | flops 1820672 | bytes 114692 | tf_op jit(solution)/shard_map/reduce-window
  12.4 0.2 copy.15
  12.5 0.1 add_bitcast_fusion
  12.7 0.7 multiply_reduce_fusion.1
  13.5 0.8 and_reduce_fusion
  14.2 0.1 reshape.362
  14.3 0.1 reshape.364
  14.4 8.8 %scatter_custom_fusion.1 = s32[2560]{0:T(1024)S(1)} fusion(s32[1600]{0:T(1024)S(1)} %reshape.362, s32[1600]{0:T(1024)S(1)} %reshape.364, s32[]{:T(128)} %constant.33.clone.1), kind=kCustom, calls=%fused_computation.54 | custom fusion | bytes 10244
  23.3 0.1 all_to_all.18
  23.4 13.6 %all_to_all.21 = s32[8,1,320]{2,1,0:T(1,128)S(1)} all-to-all(s32[8,1,320]{2,1,0:T(1,128)S(1)} %all_to_all.18), channel_id=1, replica_groups=mesh['groups'=2,'rows'=8,'cols'=2] {'rows'}, dimensions={0} | all-to-all | bytes 20480 | tf_op jit(solution)/shard_map/all_to_all | solution.py:72
  37.2 10.5 %gather_fusion = bf16[2560,512]{1,0:T(8,128)(2,1)} fusion(f32[2048,512]{1,0:T(8,128)} %param.7, s32[3072]{0:T(1024)S(1)} %pad_clamp_fusion), kind=kCustom, calls=%fused_computation | custom fusion | bytes 5253120 | tf_op jit(solution)/shard_map/jit(_take)/gather | solution.py:70
  47.7 3.2 %select_convert_fusion = bf16[8,320,512]{2,1,0:T(8,128)(2,1)} fusion(bf16[8,320,512]{2,1,0:T(8,128)(2,1)} %bitcast.25, pred[8,320]{1,0:T(8,128)(4,1)S(1)} %compare_and_fusion), kind=kLoop, calls=%fused_computation.3 | loop fusion | flops 1310720 | bytes 5245440 | tf_op jit(solution)/shard_map/convert_element_type | solution.py:76
  50.9 4.5 %all-to-all-start.1 = ((bf16[8,320,512]{2,1,0:T(8,128)(2,1)}), bf16[8,320,512]{2,1,0:T(8,128)(2,1)}, u32[]{:S(2)}, u32[]{:S(2)}) async-start(bf16[8,320,512]{2,1,0:T(8,128)(2,1)} %select_convert_fusion), calls=%async_computation.1 | async-start | bytes 5242880 | tf_op jit(solution)/shard_map/all_to_all | solution.py:75
  55.5 0.1 reduce_sum.32
  55.6 0.1 reshape_reshape.7
  55.8 0.1 add.183
  56.0 0.1 add.187
  56.1 0.1 reduce_sum.33
  56.2 0.1 broadcast_divide_fusion
  56.3 0.1 reshape.358
  56.5 0.1 multiply_reduce_fusion.2
  56.6 0.1 and_reduce_fusion.1
  56.7 10.1 %scatter_custom_fusion = f32[81920]{0:T(1024)S(1)} fusion(s32[1600]{0:T(1024)S(1)} %broadcast_select_fusion, f32[1600]{0:T(1024)S(1)} %reshape.358, f32[]{:T(128)} %constant.24.clone.1), kind=kCustom, calls=%fused_computation.6 | custom fusion | flops 1600 | bytes 327684
  66.9 0.3 fusion.4
  67.2 46.6 %all-to-all-done.1 = bf16[8,320,512]{2,1,0:T(8,128)(2,1)} async-done(((bf16[8,320,512]{2,1,0:T(8,128)(2,1)}), bf16[8,320,512]{2,1,0:T(8,128)(2,1)}, u32[]{:S(2)}, u32[]{:S(2)}) %all-to-all-start.1) | async-done | bytes 2621472 | tf_op jit(solution)/shard_map/all_to_all | solution.py:75
  113.8 3.1 %convolution_convert_fusion = bf16[32,512]{1,0:T(8,128)(2,1)S(1)} fusion(f32[32,2560]{1,0:T(8,128)S(1)} %reshape.342, bf16[2560,512]{1,0:T(8,128)(2,1)} %bitcast.8), kind=kOutput, calls=%fused_computation.5 | convolution fusion | flops 503332864 | bytes 2981888 | tf_op jit(solution)/shard_map/dot_general | solution.py:78
  116.9 0.9 convolution_add_fusion
  117.9 17.1 %all-reduce.3.cloned.1.call-done = f32[32,1024]{1,0:T(8,128)} async-done(((f32[32,1024]{1,0:T(8,128)}), f32[32,1024]{1,0:T(8,128)}) %all-reduce.3.cloned.1.call-update) | async-done | bytes 131088 | tf_op jit(solution)/shard_map/psum | solution.py:88
  135.0 1.0 multiply_reduce_fusion
  136.0 0.7 dynamic-slice_multiply_fusion
  (44 shorter events, 0.8 us)
Async XLA Ops:
  6.5 60.3 %copy-start = (bf16[512,1024]{1,0:T(8,128)(2,1)S(1)}, bf16[512,1024]{1,0:T(8,128)(2,1)}, u32[]{:S(2)}) copy-start(bf16[512,1024]{1,0:T(8,128)(2,1)} %param.11) | copy-start | bytes 3145732
  50.9 4.7 %copy-start.2 = (s32[32,50]{1,0:T(8,128)S(1)}, s32[32,50]{1,0:T(8,128)}, u32[]{:S(2)}) copy-start(s32[32,50]{1,0:T(8,128)} %param.9) | copy-start | bytes 19204
  50.9 5.2 %copy-start.4 = (f32[32,50]{1,0:T(8,128)S(1)}, f32[32,50]{1,0:T(8,128)}, u32[]{:S(2)}) copy-start(f32[32,50]{1,0:T(8,128)} %param.10) | copy-start | bytes 19204
  50.9 5.5 %copy-start.7 = (s32[2]{0:T(128)S(1)}, s32[2]{0:T(128)}, u32[]{:S(2)}) copy-start(s32[2]{0:T(128)} %constant.81) | copy-start | bytes 28
  50.9 5.6 %copy-start.6 = (s32[2]{0:T(128)S(1)}, s32[2]{0:T(128)}, u32[]{:S(2)}) copy-start(s32[2]{0:T(128)} %constant.84) | copy-start | bytes 28
  50.9 15.9 %copy-start.3 = (f32[32,512]{1,0:T(8,128)S(1)}, f32[32,512]{1,0:T(8,128)}, u32[]{:S(2)}) copy-start(f32[32,512]{1,0:T(8,128)} %param.8) | copy-start | bytes 196612
  50.9 62.9 %all-to-all-start.1 = ((bf16[8,320,512]{2,1,0:T(8,128)(2,1)}), bf16[8,320,512]{2,1,0:T(8,128)(2,1)}, u32[]{:S(2)}, u32[]{:S(2)}) async-start(bf16[8,320,512]{2,1,0:T(8,128)(2,1)} %select_convert_fusion), calls=%async_computation.1 | async-start | bytes 5242880 | tf_op jit(solution)/shard_map/all_to_all | solution.py:75
  55.5 79.5 %all-reduce.3.cloned.1.call-start = ((), (), s32[]{:S(2)}) async-start(), calls=%async_computation.2 | async-start | bytes 262144 | tf_op jit(solution)/shard_map/psum | solution.py:88
  56.6 60.3 %copy-start.1 = (bf16[512,1024]{1,0:T(8,128)(2,1)S(1)}, bf16[512,1024]{1,0:T(8,128)(2,1)}, u32[]{:S(2)}) copy-start(bf16[512,1024]{1,0:T(8,128)(2,1)} %param.12) | copy-start | bytes 3145732
  66.9 68.1 %copy-start.5 = (f32[1024]{0:T(1024)S(1)}, f32[1024]{0:T(1024)}, u32[]{:S(2)}) copy-start(f32[1024]{0:T(1024)} %param.13) | copy-start | bytes 12292
Sparse Core Ops, SparseCore 0:
  118.0 16.9 all-reduce.2
where the time goes:
time: 144 us
  waiting for transfers between devices  63.8 us (44%)
  local copies, waits for them, and re-layouts  22.4 us (16%)
  other arithmetic  21.3 us (15%)
  blocking collectives  13.6 us (9%)
  between operations  13.6 us (9%)
  starting transfers between devices  4.58 us (3%)
  matrix products  4.29 us (3%)
    all_to_all x1, waiting for transfers between devices, body(): lax.all_to_all(found.astype(jnp.bfloat16), 'rows', split_axis=0, concat_a...  46.6 us
    psum x1, waiting for transfers between devices, body(): preact = lax.psum(partial_sums, 'cols') + bias  17.1 us
    all_to_all x1, blocking collectives, body(): lax.all_to_all(outgoing, 'rows', split_axis=0, concat_axis=0, tiled=True)  13.6 us
    unnamed x7, other arithmetic  11.8 us
    gather x1, local copies, waits for them, and re-layouts, body(): jnp.take(feature_table, lax.all_to_all(outgoing, 'rows', split_axis=0, co...  10.5 us
    unnamed x19, local copies, waits for them, and re-layouts  8.94 us
    all_to_all x1, starting transfers between devices, body(): lax.all_to_all(found.astype(jnp.bfloat16), 'rows', split_axis=0, concat_a...  4.54 us
    another operation x4, other arithmetic  4.06 us
  transfers between devices with their start and end apart: 2, of which 2 were waited for; matrix products, arithmetic and copies ran while one was open for 8% of the time, Pallas kernels for 0%

commit v1 on v0

--- a/solution.py
+++ b/solution.py
@@ -85,7 +85,7 @@
         pooled.astype(jnp.bfloat16), w_pool, preferred_element_type=jnp.float32
     )
     column_start = lax.axis_index("cols") * width_half
-    preact = lax.psum(partial_sums, "cols") + bias
+    preact = jnp.sum(lax.all_gather(partial_sums, "cols"), axis=0) + bias
     embedded = finish_rows(preact)
     return lax.dynamic_slice_in_dim(embedded, column_start, width_half, 1)
 

time: 144 us -> 114 us (0.79)
  waiting for transfers between devices: 63.8 us -> 46.7 us
  between operations: 13.6 us -> 0.26 us
  blocking collectives: 13.6 us -> 15.6 us
    psum x1 -> x0, waiting for transfers between devices: 17.1 us -> none  [body(): preact = lax.psum(partial_sums, 'cols') + bias]
    all_gather x0 -> x1, blocking collectives: none -> 1.99 us  [body(): preact = jnp.sum(lax.all_gather(partial_sums, 'cols'), axis=0) + bias]
  transfers between devices with their start and end apart: 2 -> 1, of which waited for: 2 -> 1; matrix products, arithmetic and copies ran while one was open for 8% -> 10% of each run, Pallas kernels for 0% -> 0%
where the time goes in v1:
time: 114 us
  waiting for transfers between devices  46.7 us (41%)
  local copies, waits for them, and re-layouts  22.3 us (20%)
  other arithmetic  20.4 us (18%)
  blocking collectives  15.6 us (14%)
  starting transfers between devices  4.54 us (4%)
  matrix products  3.63 us (3%)
    all_to_all x1, waiting for transfers between devices, body(): lax.all_to_all(found.astype(jnp.bfloat16), 'rows', split_axis=0, concat_a...  46.7 us
    all_to_all x1, blocking collectives, body(): lax.all_to_all(outgoing, 'rows', split_axis=0, concat_axis=0, tiled=True)  13.6 us
    unnamed x7, other arithmetic  11.8 us
    gather x1, local copies, waits for them, and re-layouts, body(): jnp.take(feature_table, lax.all_to_all(outgoing, 'rows', split_axis=0, co...  10.5 us
    unnamed x19, local copies, waits for them, and re-layouts  8.93 us
    all_to_all x1, starting transfers between devices, body(): lax.all_to_all(found.astype(jnp.bfloat16), 'rows', split_axis=0, concat_a...  4.54 us
    another operation x4, other arithmetic  4.06 us
    convert_element_type x1, other arithmetic, body(): found.astype(jnp.bfloat16)  3.2 us
  transfers between devices with their start and end apart: 1, of which 1 were waited for; matrix products, arithmetic and copies ran while one was open for 10% of the time, Pallas kernels for 0%

profile of v1, /device:TPU:0, one launch (start us, length us, event | category | flops | bytes accessed | tf_op | source)
XLA Modules:
  0.0 113.5 jit_solution(12359786787237328707)
XLA Ops:
  0.0 0.9 reshape_reshape.8
  0.9 0.8 reshape_reshape.9
  1.8 4.0 %reduce-window.6 = s32[2,8,7,128]{3,1,2,0:T(8,128)S(1)} reduce-window(s32[2,8,7,128]{3,1,2,0:T(8,128)S(1)} %convert_bitcast_fusion, s32[]{:T(128)} %constant.33.clone.1), window={size=1x1x1x128 pad=0_0x0_0x0_0x127_0}, to_apply=%region_0.0 | reduce-window | flops 1820672 | bytes 114692 | tf_op jit(solution)/shard_map/reduce-window
  5.8 0.2 copy.15
  6.0 0.1 add_bitcast_fusion
  6.2 0.7 multiply_reduce_fusion.1
  6.9 0.8 and_reduce_fusion
  7.7 0.1 reshape.362
  7.8 0.1 reshape.364
  7.9 8.8 %scatter_custom_fusion.1 = s32[2560]{0:T(1024)S(1)} fusion(s32[1600]{0:T(1024)S(1)} %reshape.362, s32[1600]{0:T(1024)S(1)} %reshape.364, s32[]{:T(128)} %constant.33.clone.1), kind=kCustom, calls=%fused_computation.54 | custom fusion | bytes 10244
  16.8 0.1 all_to_all.18
  16.9 13.6 %all_to_all.21 = s32[8,1,320]{2,1,0:T(1,128)S(1)} all-to-all(s32[8,1,320]{2,1,0:T(1,128)S(1)} %all_to_all.18), channel_id=1, replica_groups=mesh['groups'=2,'rows'=8,'cols'=2] {'rows'}, dimensions={0} | all-to-all | bytes 20480 | tf_op jit(solution)/shard_map/all_to_all | solution.py:72
  30.6 10.5 %gather_fusion = bf16[2560,512]{1,0:T(8,128)(2,1)} fusion(f32[2048,512]{1,0:T(8,128)} %param.7, s32[3072]{0:T(1024)S(1)} %pad_clamp_fusion), kind=kCustom, calls=%fused_computation | custom fusion | bytes 5253120 | tf_op jit(solution)/shard_map/jit(_take)/gather | solution.py:70
  41.2 3.2 %select_convert_fusion = bf16[8,320,512]{2,1,0:T(8,128)(2,1)} fusion(bf16[8,320,512]{2,1,0:T(8,128)(2,1)} %bitcast.26, pred[8,320]{1,0:T(8,128)(4,1)S(1)} %compare_and_fusion), kind=kLoop, calls=%fused_computation.3 | loop fusion | flops 1310720 | bytes 5245440 | tf_op jit(solution)/shard_map/convert_element_type | solution.py:76
  44.4 4.5 %all-to-all-start.1 = ((bf16[8,320,512]{2,1,0:T(8,128)(2,1)}), bf16[8,320,512]{2,1,0:T(8,128)(2,1)}, u32[]{:S(2)}, u32[]{:S(2)}) async-start(bf16[8,320,512]{2,1,0:T(8,128)(2,1)} %select_convert_fusion), calls=%async_computation.1 | async-start | bytes 5242880 | tf_op jit(solution)/shard_map/all_to_all | solution.py:75
  49.0 0.1 reduce_sum.41
  49.0 0.1 reshape_reshape.7
  49.3 0.1 add.181
  49.4 0.1 add.185
  49.5 0.1 reduce_sum.42
  49.6 0.1 broadcast_divide_fusion
  49.7 0.1 reshape.358
  49.9 0.1 multiply_reduce_fusion.2
  50.0 0.1 and_reduce_fusion.1
  50.1 10.1 %scatter_custom_fusion = f32[81920]{0:T(1024)S(1)} fusion(s32[1600]{0:T(1024)S(1)} %broadcast_select_fusion, f32[1600]{0:T(1024)S(1)} %reshape.358, f32[]{:T(128)} %constant.24.clone.1), kind=kCustom, calls=%fused_computation.6 | custom fusion | flops 1600 | bytes 327684
  60.3 0.3 fusion.4
  60.6 46.7 %all-to-all-done.1 = bf16[8,320,512]{2,1,0:T(8,128)(2,1)} async-done(((bf16[8,320,512]{2,1,0:T(8,128)(2,1)}), bf16[8,320,512]{2,1,0:T(8,128)(2,1)}, u32[]{:S(2)}, u32[]{:S(2)}) %all-to-all-start.1) | async-done | bytes 2621472 | tf_op jit(solution)/shard_map/all_to_all | solution.py:75
  107.3 3.1 %convolution_convert_fusion = bf16[32,512]{1,0:T(8,128)(2,1)S(1)} fusion(f32[32,2560]{1,0:T(8,128)S(1)} %reshape.342, bf16[2560,512]{1,0:T(8,128)(2,1)} %bitcast.8), kind=kOutput, calls=%fused_computation.5 | convolution fusion | flops 503332864 | bytes 2981888 | tf_op jit(solution)/shard_map/dot_general | solution.py:78
  110.4 0.3 convolution_add_fusion
  110.6 2.0 %all-gather = f32[64,1024]{1,0:T(8,128)S(1)} all-gather(f32[32,1024]{1,0:T(8,128)S(1)} %convolution_add_fusion), channel_id=2, replica_groups=mesh['groups'=2,'rows'=8,'cols'=2] {'cols'}, dimensions={0}, use_global_device_ids=true | all-gather | bytes 393216 | tf_op jit(solution)/shard_map/all_gather | solution.py:88
  112.7 0.1 multiply_reduce_fusion
  112.8 0.7 dynamic-slice_multiply_fusion
  (43 shorter events, 0.8 us)
Async XLA Ops:
  0.0 60.3 %copy-start = (bf16[512,1024]{1,0:T(8,128)(2,1)S(1)}, bf16[512,1024]{1,0:T(8,128)(2,1)}, u32[]{:S(2)}) copy-start(bf16[512,1024]{1,0:T(8,128)(2,1)} %param.11) | copy-start | bytes 3145732
  44.4 4.7 %copy-start.2 = (s32[32,50]{1,0:T(8,128)S(1)}, s32[32,50]{1,0:T(8,128)}, u32[]{:S(2)}) copy-start(s32[32,50]{1,0:T(8,128)} %param.9) | copy-start | bytes 19204
  44.4 5.1 %copy-start.4 = (f32[32,50]{1,0:T(8,128)S(1)}, f32[32,50]{1,0:T(8,128)}, u32[]{:S(2)}) copy-start(f32[32,50]{1,0:T(8,128)} %param.10) | copy-start | bytes 19204
  44.4 5.5 %copy-start.7 = (s32[2]{0:T(128)S(1)}, s32[2]{0:T(128)}, u32[]{:S(2)}) copy-start(s32[2]{0:T(128)} %constant.81) | copy-start | bytes 28
  44.4 5.6 %copy-start.6 = (s32[2]{0:T(128)S(1)}, s32[2]{0:T(128)}, u32[]{:S(2)}) copy-start(s32[2]{0:T(128)} %constant.84) | copy-start | bytes 28
  44.4 15.9 %copy-start.3 = (f32[32,512]{1,0:T(8,128)S(1)}, f32[32,512]{1,0:T(8,128)}, u32[]{:S(2)}) copy-start(f32[32,512]{1,0:T(8,128)} %param.8) | copy-start | bytes 196612
  44.4 62.9 %all-to-all-start.1 = ((bf16[8,320,512]{2,1,0:T(8,128)(2,1)}), bf16[8,320,512]{2,1,0:T(8,128)(2,1)}, u32[]{:S(2)}, u32[]{:S(2)}) async-start(bf16[8,320,512]{2,1,0:T(8,128)(2,1)} %select_convert_fusion), calls=%async_computation.1 | async-start | bytes 5242880 | tf_op jit(solution)/shard_map/all_to_all | solution.py:75
  50.1 60.2 %copy-start.1 = (bf16[512,1024]{1,0:T(8,128)(2,1)S(1)}, bf16[512,1024]{1,0:T(8,128)(2,1)}, u32[]{:S(2)}) copy-start(bf16[512,1024]{1,0:T(8,128)(2,1)} %param.12) | copy-start | bytes 3145732
  60.6 52.1 %copy-start.5 = (f32[1024]{0:T(1024)S(1)}, f32[1024]{0:T(1024)}, u32[]{:S(2)}) copy-start(f32[1024]{0:T(1024)} %param.13) | copy-start | bytes 12292
